TPU v7x, 32 devices: a whole 2x2x4 slice. The times are simulated.
32 devices in a mesh: occ: 2 (over x), vir: 4 (over z), aux: 4 (over y, core).
Axes of the slice: x: 2, y: 2, z: 4, core: 2. Of those that a mesh axis runs over, the one named last changes fastest.
Arguments:
- amplitudes: bfloat16 [16, 1024, 1024], P('occ', 'vir'), may hold values from -6 to 6
- pair_mask: int32 [16, 8, 8], P('occ', 'vir'), may hold values 0 or 1
- left_factor: bfloat16 [32, 1024, 4096], P(None, 'vir', 'aux'), may hold values from -0.0390625 to 0.0390625
- left_mask: int32 [8, 32], P('vir', 'aux'), may hold values 0 or 1
- right_factor: bfloat16 [1024, 4, 4096], P(('occ', 'vir'), None, 'aux'), may hold values from -0.0390625 to 0.0390625
- right_mask: int32 [8, 32], P(None, 'aux'), may hold values 0 or 1
- residual_in: float32 [16, 4, 32], P('occ'), may hold values from -6 to 6
Outputs:
- updated: float32 [16, 4, 32], P('occ')
All inputs are finite; a program needn't handle non-finite values. No bound on the sum of `pair_mask` or of `left_mask` or of `right_mask` on one device may be relied on, other than what follows from the above.
Results may differ from a plain program's by a relative error of at most 0.0003.
Values may be sent and summed in bfloat16 or wider, within the bound.
A program may use at most 128 MiB of HBM per device.

v0:
```python
import functools

import jax
import jax.numpy as jnp
from jax import lax
from jax.experimental import pallas as pl
from jax.experimental.pallas import tpu as pltpu
from jax.sharding import PartitionSpec as P

TILE = 128
QC = 256
CC = 32
MESH = pl.DeviceIdType.MESH
F32 = jnp.float32
BF16 = jnp.bfloat16


def kernel(
    no, nv, na, pair_mask, left_mask, right_mask, amp_hbm, left_hbm, right_hbm, res,
    out, amp, left, rbuf, wr, tau, tsend, lhs2, rhs2, acc, part, parts,
    amp_sem, left_sem, own_sem, r_send, r_recv, t_send, t_recv, a_send, a_recv,
):
    occ, vir, aux = lax.axis_index("occ"), lax.axis_index("vir"), lax.axis_index("aux")
    pairs, cols, virt = amp.shape
    nq, _, bq = right_hbm.shape
    rows = rbuf.shape[2]
    block_b = bq // QC
    block_a = left.shape[0]
    cq, depth = tau.shape[3], tau.shape[4]
    pall = no * pairs
    steps = cols // CC
    subs = cq // CC
    groups = CC // 8

    def right_copy(u, n, down, own):
        src = right_hbm.at[n] if own else rbuf.at[u, n]
        return pltpu.make_async_remote_copy(
            src_ref=src,
            dst_ref=rbuf.at[u, n],
            send_sem=r_send.at[1 if down else 0, u, n],
            recv_sem=r_recv.at[u, n],
            device_id={"vir": vir - 1 if down else vir + 1},
            device_id_type=MESH,
        )

    def send_own(n):
        @pl.when(vir > 0)
        def _():
            right_copy(vir, n, True, True).start()

        @pl.when(vir < nv - 1)
        def _():
            right_copy(vir, n, False, True).start()

    def arrive(k, n, forwarded):
        for down in (True, False):
            u = vir + k if down else vir - k
            here = u < nv if down else u >= 0
            passes = vir > 0 if down else vir < nv - 1

            @pl.when(here & (passes if forwarded else jnp.logical_not(passes)))
            def _():
                right_copy(u, n, down, False).wait_recv()
                if forwarded:
                    right_copy(u, n, down, False).start()

    amp_copy = pltpu.make_async_copy(amp_hbm, amp, amp_sem)
    amp_copy.start()
    send_own(0)
    if nq > 1:
        send_own(1)
    own_copies = [
        pltpu.make_async_copy(right_hbm.at[n], rbuf.at[vir, n], own_sem.at[n]) for n in range(nq)
    ]
    for copy in own_copies:
        copy.start()

    def left_copy(n):
        return pltpu.make_async_copy(
            left_hbm.at[:, :, pl.ds(pl.multiple_of(n * QC, QC), QC)],
            left.at[:, :, pl.ds(pl.multiple_of(n * QC, QC), QC)],
            left_sem.at[n],
        )

    for n in range(nq):
        left_copy(n).start()
    amp_copy.wait()

    piece = min(cq, TILE)

    def masked(p, row, column):
        m = pair_mask[p, row // TILE, column // TILE].astype(F32)
        block = amp[
            p, pl.ds(pl.multiple_of(row, piece), piece), pl.ds(pl.multiple_of(column, TILE), TILE)
        ]
        return (block.astype(F32) * m).astype(BF16)

    def fill_send(p, carry):
        for k in range(1, no):
            base = lax.rem(occ + k, no) * depth
            for off in range(0, cq, piece):
                for col in range(0, depth, TILE):
                    tsend[k - 1, p, off : off + piece, col : col + TILE] = masked(
                        p, aux * cq + off, base + col
                    )
        return carry

    lax.fori_loop(0, pairs, fill_send, 0)

    def tau_copy(k, sem, q, src, device):
        slot = lax.rem(occ + k, no)
        return pltpu.make_async_remote_copy(
            src_ref=src,
            dst_ref=tau.at[slot, q],
            send_sem=t_send.at[k, sem],
            recv_sem=t_recv.at[slot, q],
            device_id=device,
            device_id_type=MESH,
        )

    def occ_copy(k):
        return pltpu.make_async_remote_copy(
            src_ref=tsend.at[k - 1],
            dst_ref=tau.at[occ, aux],
            send_sem=t_send.at[k, 0],
            recv_sem=t_recv.at[occ, aux],
            device_id={"occ": lax.rem(occ + k, no)},
            device_id_type=MESH,
        )

    acc[...] = jnp.zeros_like(acc)
    for k in range(1, no):
        occ_copy(k).start()

    def fill_own(i, carry):
        p, q = i // na, lax.rem(i, na)
        for off in range(0, cq, piece):
            for col in range(0, depth, TILE):
                tau[occ, q, p, off : off + piece, col : col + TILE] = masked(
                    p, q * cq + off, occ * depth + col
                )
        return carry

    lax.fori_loop(0, pairs * na, fill_own, 0)

    bits = []
    bit = na // 2
    while bit:
        bits.append(bit)
        bit //= 2
    have = [0]
    sent = 1
    tau_sends = [occ_copy(k) for k in range(1, no)]
    waves = list(range(1, nv))
    arrive(1, 0, True)
    for stage, bit in enumerate(bits):
        for k in range(1, no):
            for m in have if stage == 0 else have[len(have) // 2 :]:
                q = aux ^ m
                tau_copy(k, 0, q, tau.at[lax.rem(occ + k, no), q], {"aux": aux ^ bit}).wait_recv()
            for i, m in enumerate(have):
                q = aux ^ m
                copy = tau_copy(
                    k, sent + i, q, tau.at[lax.rem(occ + k, no), q], {"aux": aux ^ bit}
                )
                copy.start()
                tau_sends.append(copy)
        sent += len(have)
        have = have + [m ^ bit for m in have]
        if stage == 0:
            for k in waves[1:]:
                arrive(k, 0, True)
            if nq > 2:
                send_own(2)
    for k in range(1, no):
        for m in have[len(have) // 2 :] if bits else have:
            q = aux ^ m
            tau_copy(k, 0, q, tau.at[lax.rem(occ + k, no), q], {"occ": lax.rem(occ + k, no)}).wait_recv()
    for copy in own_copies:
        copy.wait()

    sub_rows = min(rows, TILE)
    lane = lax.broadcasted_iota(jnp.int32, (1, QC), 1)

    def step(it, carry):
        n = it // steps
        cs = lax.rem(it, steps)

        @pl.when(cs == 0)
        def _():
            for k in waves:
                arrive(k, n, False)
            left_copy(n).wait()
            for u in range(nv):
                for r in range(0, rows, sub_rows):
                    dt = (occ * depth + u * rows + r) // TILE
                    m = jnp.zeros((1, QC), F32)
                    for t in range(QC // TILE):
                        m = jnp.where(
                            lane // TILE == t, right_mask[dt, n * (QC // TILE) + t].astype(F32), m
                        )
                    for b in range(block_b):
                        x = rbuf[u, n, pl.ds(r, sub_rows), b * QC : (b + 1) * QC]
                        wr[u * rows + r : u * rows + r + sub_rows, b * QC : (b + 1) * QC] = (
                            x.astype(F32) * m
                        ).astype(BF16)

        for k in waves:
            @pl.when((cs == min(2 * k, steps - 1)) & (n + 1 < nq))
            def _():
                arrive(k, n + 1, True)
                if k == nv - 1:
                    @pl.when(n + 3 < nq)
                    def _():
                        send_own(n + 3)

        c0 = pl.multiple_of(cs * CC, CC)
        q0 = pl.multiple_of(n * QC, QC)
        lm = jnp.zeros((1, QC), F32)
        for t in range(QC // TILE):
            lm = jnp.where(
                lane // TILE == t, left_mask[cs * CC // TILE, n * (QC // TILE) + t].astype(F32), lm
            )
        w = left[:, pl.ds(c0, CC), pl.ds(q0, QC)].astype(F32) * lm[None]
        w = w.reshape(block_a, groups, 8, QC)
        for j in range(groups):
            rhs2[:, j * QC : (j + 1) * QC] = w[:, j].reshape(block_a * 8, QC).astype(BF16)
        q, s = cs // subs, lax.rem(cs, subs)
        t = tau[:, q, :, pl.ds(pl.multiple_of(s * CC, CC), CC), :].reshape(pall * CC, depth)
        half = pall * 8
        for b in range(block_b):
            inner = jnp.dot(t, wr[:, b * QC : (b + 1) * QC], preferred_element_type=F32)
            inner = inner.reshape(pall, groups, 8, QC)
            for j in range(groups):
                x = inner[:, j].reshape(half, QC)
                hi = x.astype(BF16)
                lo = (x - hi.astype(F32)).astype(BF16)
                lhs2[2 * b * half : (2 * b + 1) * half, j * QC : (j + 1) * QC] = hi
                lhs2[(2 * b + 1) * half : (2 * b + 2) * half, j * QC : (j + 1) * QC] = lo
            sl = slice(2 * b * half, (2 * b + 2) * half)
            acc[sl, :] += lax.dot_general(
                lhs2[sl, :], rhs2[...], (((1,), (1,)), ((), ())), preferred_element_type=F32
            )
        return carry

    lax.fori_loop(0, nq * steps, step, 0)

    half = pall * 8
    width = block_a * 8
    row_i = lax.rem(lax.broadcasted_iota(jnp.int32, (half, width), 0), 8)
    col_i = lax.rem(lax.broadcasted_iota(jnp.int32, (half, width), 1), 8)
    diag = (row_i == col_i).astype(F32)
    total = jnp.zeros((pall, block_b * block_a), F32)
    src = lax.broadcasted_iota(jnp.int32, (width, block_b * block_a), 0) // 8
    dst = lax.broadcasted_iota(jnp.int32, (width, block_b * block_a), 1)
    for b in range(block_b):
        y = acc[2 * b * half : (2 * b + 1) * half, :] + acc[(2 * b + 1) * half : (2 * b + 2) * half, :]
        y = (y * diag).reshape(pall, 8, width).sum(axis=1)
        pick = (src + b * block_a == dst).astype(F32)
        total += jnp.dot(y, pick, precision=lax.Precision.HIGHEST, preferred_element_type=F32)
    part[...] = total.reshape(no, pairs, block_b * block_a)

    devices = no * nv * na
    me = (occ * nv + vir) * na + aux
    parts[me] = part[occ]

    def final_copy(k):
        j = lax.rem(me + k, devices)
        to = (j // (nv * na), lax.rem(j // na, nv), lax.rem(j, na))
        return pltpu.make_async_remote_copy(
            src_ref=part.at[to[0]],
            dst_ref=parts.at[me],
            send_sem=a_send.at[k],
            recv_sem=a_recv.at[me],
            device_id=to,
            device_id_type=MESH,
        )

    def final_arrival(k):
        j = lax.rem(me + k, devices)
        to = (j // (nv * na), lax.rem(j // na, nv), lax.rem(j, na))
        return pltpu.make_async_remote_copy(
            src_ref=part.at[to[0]],
            dst_ref=parts.at[j],
            send_sem=a_send.at[k],
            recv_sem=a_recv.at[j],
            device_id=to,
            device_id_type=MESH,
        )

    def start_final(k, carry):
        final_copy(k).start()
        return carry

    def wait_final(k, carry):
        final_arrival(k).wait_recv()
        return carry

    def drain_final(k, carry):
        final_copy(k).wait_send()
        return carry

    lax.fori_loop(1, devices, start_final, 0)
    for copy in tau_sends:
        copy.wait_send()
    for n in range(nq):
        for down in (True, False):
            passes = vir > 0 if down else vir < nv - 1

            @pl.when(passes)
            def _():
                right_copy(vir, n, down, True).wait_send()

            for k in waves:
                u = vir + k if down else vir - k
                here = u < nv if down else u >= 0

                @pl.when(passes & here)
                def _():
                    right_copy(u, n, down, False).wait_send()
    lax.fori_loop(1, devices, wait_final, 0)
    out[...] = res[...] + jnp.sum(parts[...], axis=0)
    lax.fori_loop(1, devices, drain_final, 0)


def local(sizes, amplitudes, pair_mask, left_factor, left_mask, right_factor, right_mask, residual_in):
    no, nv, na = sizes
    pairs, cols, virt = amplitudes.shape
    rows, block_b, auxn = right_factor.shape
    block_a = left_factor.shape[0]
    nq = auxn // QC
    depth = rows * nv
    cq = cols // na
    pall = no * pairs
    right = right_factor.reshape(rows, block_b, nq, QC).transpose(2, 0, 1, 3)
    right = right.reshape(nq, rows, block_b * QC)
    ba = block_b * block_a
    vmem = pl.BlockSpec(memory_space=pltpu.VMEM)
    smem = pl.BlockSpec(memory_space=pltpu.SMEM)
    hbm = pl.BlockSpec(memory_space=pltpu.MemorySpace.HBM)
    dma = pltpu.SemaphoreType.DMA
    out = pl.pallas_call(
        functools.partial(kernel, no, nv, na),
        out_shape=jax.ShapeDtypeStruct((pairs, ba), F32),
        in_specs=[smem, smem, smem, hbm, hbm, hbm, vmem],
        out_specs=vmem,
        scratch_shapes=[
            pltpu.VMEM((pairs, cols, virt), BF16),
            pltpu.VMEM(left_factor.shape, BF16),
            pltpu.VMEM((nv, nq, rows, block_b * QC), BF16),
            pltpu.VMEM((depth, block_b * QC), BF16),
            pltpu.VMEM((no, na, pairs, cq, depth), BF16),
            pltpu.VMEM((max(no - 1, 1), pairs, cq, depth), BF16),
            pltpu.VMEM((2 * block_b * pall * 8, CC // 8 * QC), BF16),
            pltpu.VMEM((block_a * 8, CC // 8 * QC), BF16),
            pltpu.VMEM((2 * block_b * pall * 8, block_a * 8), F32),
            pltpu.VMEM((no, pairs, ba), F32),
            pltpu.VMEM((no * nv * na, pairs, ba), F32),
            dma,
            dma((nq,)),
            dma((nq,)),
            dma((2, nv, nq)),
            dma((nv, nq)),
            dma((no, na)),
            dma((no, na)),
            dma((no * nv * na,)),
            dma((no * nv * na,)),
        ],
        compiler_params=pltpu.CompilerParams(
            has_side_effects=True, vmem_limit_bytes=62 * 1024 * 1024
        ),
        name="ladder",
    )(pair_mask, left_mask, right_mask, amplitudes, left_factor, right,
      residual_in.reshape(pairs, ba))
    return out.reshape(pairs, block_b, block_a)


def solution(mesh):
    sizes = tuple(mesh.shape[name] for name in ("occ", "vir", "aux"))
    return jax.shard_map(
        functools.partial(local, sizes),
        mesh=mesh,
        in_specs=(
            P("occ", "vir", None),
            P("occ", "vir", None),
            P(None, "vir", "aux"),
            P("vir", "aux"),
            P(("occ", "vir"), None, "aux"),
            P(None, "aux"),
            P("occ", None, None),
        ),
        out_specs=P("occ", None, None),
        check_vma=False,
    )
```

profile of v0, /device:TPU:0, one launch (start us, length us, event | category | flops | bytes accessed | tf_op | source)
XLA Modules:
  0.0 118.8 jit_solution(8865320359938048704)
XLA Ops:
  0.0 1.6 %copy.11 = bf16[128,1,4,4,256]{4,3,1,0,2:T(4,128)(2,1)S(1)} copy(bf16[128,1,4,4,256]{4,3,2,1,0:T(4,128)(2,1)} %bitcast.8) | data formatting | bytes 2097152 | tf_op jit(solution)/shard_map/reshape | solution.py:335
  1.6 1.6 %reshape.13.right_hbm = bf16[4,128,1024]{2,1,0:T(8,128)(2,1)} reshape(bf16[4,128,4,256]{3,2,1,0:T(4,128)(2,1)S(1)} %bitcast.7) | data formatting | bytes 2097152 | tf_op jit(solution)/shard_map/reshape | solution.py:336
  3.2 1.4 %reshape.14.res = f32[8,128]{1,0:T(8,128)} reshape(f32[8,4,32]{2,1,0:T(4,128)} %param.13) | data formatting | bytes 8192 | tf_op jit(solution)/shard_map/reshape | solution.py:374
  4.5 112.9 %ladder.1 = f32[8,128]{1,0:T(8,128)} custom-call(s32[8,2,8]{2,1,0:T(2,128)} %pair_mask.1, s32[2,8]{1,0:T(2,128)} %left_mask.1, s32[8,8]{1,0:T(8,128)} %right_mask.1, bf16[8,256,1024]{2,1,0:T(8,128)(2,1)} %amp_hbm.1, bf16[32,256,1024]{2,1,0:T(8,128)(2,1)} %left_hbm.1, bf16[4,128,1024]{2,1,0:T(8,128)(2,1)} %reshape.13.right_hbm, f32[8,128]{1,0:T(8,128)} %reshape.14.res), custom_call_target="tpu_custom_call" | custom-call | tf_op jit(solution)/shard_map/ladder/pallas_call | solution.py:342
  117.4 1.4 %reshape.15 = f32[8,4,32]{2,1,0:T(4,128)} reshape(f32[8,128]{1,0:T(8,128)} %ladder.1) | data formatting | bytes 8192 | tf_op jit(solution)/shard_map/reshape | solution.py:375
where the time goes:
time: 119 us
  Pallas kernels  113 us (95%)
  local copies, waits for them, and re-layouts  5.9 us (5%)
    pallas_call x1, Pallas kernels, local(): pl.pallas_call(functools.partial(kernel, no, nv, na), out_shape=jax.Shape...  113 us

commit v1 on v0

v1 whole, which is shorter than its diff:
```python
import functools

import jax
import jax.numpy as jnp
from jax import lax
from jax.experimental import pallas as pl
from jax.experimental.pallas import tpu as pltpu
from jax.sharding import PartitionSpec as P

TILE = 128
QC = 128
CC = 32
AHEAD = 4
MESH = pl.DeviceIdType.MESH
F32 = jnp.float32
BF16 = jnp.bfloat16


def kernel(
    no, nv, na, pair_mask, left_mask, right_mask, amp_hbm, left_hbm, right_hbm, res,
    out, raw, amp, left, rbuf, tau, tsend, lhs_a, rhs_a, lhs_b, rhs_b, acc, part, parts,
    amp_sem, left_sem, raw_sem, r_send, r_recv, t_send, t_recv, a_send, a_recv, enter,
):
    occ, vir, aux = lax.axis_index("occ"), lax.axis_index("vir"), lax.axis_index("aux")
    pairs, cols, virt = amp.shape
    nq, _, rows, bq = rbuf.shape
    block_b = bq // QC
    block_a = left.shape[0]
    cq, depth = tau.shape[3], tau.shape[4]
    pall = no * pairs
    steps = cols // CC
    subs = cq // CC
    groups = CC // 8
    half = pall * 8
    pieces = min(4, pairs)
    pp = pairs // pieces
    waves = list(range(1, nv))
    lead = max(3, nv - 2)

    place = {"occ": (occ, no), "vir": (vir, nv), "aux": (aux, na)}

    def greet(sem, axes):
        count = 0
        for axis in axes:
            at, size = place[axis]
            for k in range(1, size):
                pl.semaphore_signal(
                    sem, inc=1, device_id={axis: lax.rem(at + k, size)}, device_id_type=MESH
                )
                count += 1
        return count

    greeted = greet(pltpu.get_barrier_semaphore(), ("occ", "vir", "aux"))
    raw_copy = pltpu.make_async_copy(right_hbm, raw, raw_sem)
    raw_copy.start()
    amp_copy = pltpu.make_async_copy(amp_hbm, amp, amp_sem)
    amp_copy.start()

    def right_copy(u, n, down):
        return pltpu.make_async_remote_copy(
            src_ref=rbuf.at[n, u],
            dst_ref=rbuf.at[n, u],
            send_sem=r_send.at[1 if down else 0, u, n],
            recv_sem=r_recv.at[u, n],
            device_id={"vir": vir - 1 if down else vir + 1},
            device_id_type=MESH,
        )

    def send_own(n):
        @pl.when(vir > 0)
        def _():
            right_copy(vir, n, True).start()

        @pl.when(vir < nv - 1)
        def _():
            right_copy(vir, n, False).start()

    def arrive(k, n, forwarded, valid=True):
        for down in (True, False):
            u = vir + k if down else vir - k
            here = u < nv if down else u >= 0
            passes = vir > 0 if down else vir < nv - 1

            @pl.when(here & (passes if forwarded else jnp.logical_not(passes)) & valid)
            def _():
                right_copy(u, n, down).wait_recv()
                if forwarded:
                    right_copy(u, n, down).start()

    def relay(k, m):
        n = m - k + 1
        if k <= nv - 2:
            if isinstance(m, int):
                if 0 <= n < nq:
                    arrive(k, n, True)
            else:
                arrive(k, n, True, (n >= 0) & (n < nq))

    def more_own(m):
        n = m + AHEAD
        if isinstance(m, int):
            if n < nq:
                send_own(n)
        else:
            @pl.when(n < nq)
            def _():
                send_own(n)

    def slot(m):
        relay(1, m)
        more_own(m)
        for k in waves[1:]:
            relay(k, m)

    def left_copy(n):
        return pltpu.make_async_copy(
            left_hbm.at[:, :, pl.ds(pl.multiple_of(n * QC, QC), QC)],
            left.at[:, :, pl.ds(pl.multiple_of(n * QC, QC), QC)],
            left_sem.at[n],
        )

    sub_rows = min(rows, TILE)
    first = (occ * nv + vir) * rows

    def arrange(n, carry):
        for r in range(0, rows, sub_rows):
            m = right_mask[(first + r) // TILE, n * QC // TILE].astype(F32)
            x = raw[pl.ds(r, sub_rows), :, pl.ds(pl.multiple_of(n * QC, QC), QC)].astype(F32) * m
            for b in range(block_b):
                rbuf[n, vir, r : r + sub_rows, b * QC : (b + 1) * QC] = x[:, b, :].astype(BF16)
        return carry

    raw_copy.wait()
    lax.fori_loop(0, nq, arrange, 0)
    amp_copy.wait()
    for n in range(nq):
        left_copy(n).start()

    piece = min(cq, TILE)

    def masked(p, row, column):
        m = pair_mask[p, row // TILE, column // TILE].astype(F32)
        block = amp[
            p, pl.ds(pl.multiple_of(row, piece), piece), pl.ds(pl.multiple_of(column, TILE), TILE)
        ]
        return (block.astype(F32) * m).astype(BF16)

    def fill_send(p, carry):
        for k in range(1, no):
            base = lax.rem(occ + k, no) * depth
            for off in range(0, cq, piece):
                for col in range(0, depth, TILE):
                    tsend[k - 1, p, off : off + piece, col : col + TILE] = masked(
                        p, aux * cq + off, base + col
                    )
        return carry

    def occ_copy(k, h):
        return pltpu.make_async_remote_copy(
            src_ref=tsend.at[k - 1, pl.ds(h * pp, pp)],
            dst_ref=tau.at[occ, aux, pl.ds(h * pp, pp)],
            send_sem=t_send.at[k, 0, h],
            recv_sem=t_recv.at[occ, aux, h],
            device_id={"occ": lax.rem(occ + k, no)},
            device_id_type=MESH,
        )

    def aux_copy(k, sem, q, h, bit):
        side = lax.rem(occ + k, no)
        block = tau.at[side, q, pl.ds(h * pp, pp)]
        return pltpu.make_async_remote_copy(
            src_ref=block,
            dst_ref=block,
            send_sem=t_send.at[k, sem, h],
            recv_sem=t_recv.at[side, q, h],
            device_id={"aux": aux ^ bit},
            device_id_type=MESH,
        )

    lax.fori_loop(0, pairs, fill_send, 0)
    pl.semaphore_wait(pltpu.get_barrier_semaphore(), greeted)
    for n in range(min(AHEAD, nq)):
        send_own(n)
    tau_sends = []
    for h in range(pieces):
        for k in range(1, no):
            copy = occ_copy(k, h)
            copy.start()
            tau_sends.append(copy)

    acc[...] = jnp.zeros_like(acc)
    lhs_b[...] = jnp.zeros_like(lhs_b)
    rhs_b[...] = jnp.zeros_like(rhs_b)

    def fill_own(i, carry):
        p, q = i // na, lax.rem(i, na)
        for off in range(0, cq, piece):
            for col in range(0, depth, TILE):
                tau[occ, q, p, off : off + piece, col : col + TILE] = masked(
                    p, q * cq + off, occ * depth + col
                )
        return carry

    lax.fori_loop(0, pairs * na, fill_own, 0)

    bits = []
    bit = na // 2
    while bit:
        bits.append(bit)
        bit //= 2

    news = [[0]]
    have = [0]
    for bit in bits:
        news.append([m ^ bit for m in have])
        have = have + news[-1]
    sems = {}
    for s in range(len(news)):
        for m in news[s]:
            for later in range(s, len(bits)):
                sems[m, later] = len(sems) + 1

    def tau_stage(s, h):
        for k in range(1, no):
            for m in news[s]:
                q = aux ^ m
                aux_copy(k, 0, q, h, 0).wait_recv()
                for later in range(s, len(bits)):
                    copy = aux_copy(k, sems[m, later], q, h, bits[later])
                    copy.start()
                    tau_sends.append(copy)

    done = 0
    for w in range(pieces + len(bits)):
        for s in range(len(news)):
            if 0 <= w - s < pieces:
                tau_stage(s, w - s)
        while done < lead and (done + 1) * (pieces + len(bits)) <= (w + 1) * lead:
            slot(done)
            done += 1
    while done < lead:
        slot(done)
        done += 1
    pl.semaphore_wait(enter.at[0], greet(enter.at[0], ("vir",)))
    pl.semaphore_wait(enter.at[1], greet(enter.at[1], ("aux",)))

    def stage_two(lhs, rhs):
        acc[...] += lax.dot_general(
            lhs[...], rhs[...], (((1,), (1,)), ((), ())), preferred_element_type=F32
        )

    def stage_one(n, cs, lhs, rhs):
        c0 = pl.multiple_of(cs * CC, CC)
        q0 = pl.multiple_of(n * QC, QC)
        lm = left_mask[cs * CC // TILE, n * QC // TILE].astype(F32)
        w = left[:, pl.ds(c0, CC), pl.ds(q0, QC)].astype(F32) * lm
        w = w.reshape(block_a, groups, 8, QC)
        for j in range(groups):
            rhs[:, j * QC : (j + 1) * QC] = w[:, j].reshape(block_a * 8, QC).astype(BF16)
        q, s = cs // subs, lax.rem(cs, subs)
        t = tau[:, q, :, pl.ds(pl.multiple_of(s * CC, CC), CC), :].reshape(pall * CC, depth)
        for b in range(0, block_b, 2):
            r = rbuf[n, :, :, b * QC : (b + 2) * QC].reshape(depth, 2 * QC)
            inner = jnp.dot(t, r, preferred_element_type=F32)
            inner = inner.reshape(pall, groups, 8, 2 * QC)
            for j in range(groups):
                for e in range(2):
                    x = inner[:, j, :, e * QC : (e + 1) * QC].reshape(half, QC)
                    hi = x.astype(BF16)
                    lo = (x - hi.astype(F32)).astype(BF16)
                    row = 2 * (b + e) * half
                    lhs[row : row + half, j * QC : (j + 1) * QC] = hi
                    lhs[row + half : row + 2 * half, j * QC : (j + 1) * QC] = lo

    turns = steps // 2

    def turn(it, carry):
        n = it // turns
        ds = lax.rem(it, turns)

        @pl.when(ds == 0)
        def _():
            for k in waves:
                arrive(k, n, False)
            left_copy(n).wait()

        for k in waves[:-1]:
            @pl.when(ds == min(k, turns - 1))
            def _():
                relay(k, n + lead)
                if k == 1:
                    more_own(n + lead)

        if nv <= 2:
            @pl.when(ds == 0)
            def _():
                more_own(n + lead)

        stage_two(lhs_b, rhs_b)
        stage_one(n, 2 * ds, lhs_a, rhs_a)
        stage_two(lhs_a, rhs_a)
        stage_one(n, 2 * ds + 1, lhs_b, rhs_b)
        return carry

    lax.fori_loop(0, nq * turns, turn, 0)
    stage_two(lhs_b, rhs_b)

    width = block_a * 8
    row_i = lax.rem(lax.broadcasted_iota(jnp.int32, (half, width), 0), 8)
    col_i = lax.rem(lax.broadcasted_iota(jnp.int32, (half, width), 1), 8)
    diag = (row_i == col_i).astype(F32)
    total = jnp.zeros((pall, block_b * block_a), F32)
    src = lax.broadcasted_iota(jnp.int32, (width, block_b * block_a), 0) // 8
    dst = lax.broadcasted_iota(jnp.int32, (width, block_b * block_a), 1)
    for b in range(block_b):
        y = acc[2 * b * half : (2 * b + 1) * half, :] + acc[(2 * b + 1) * half : (2 * b + 2) * half, :]
        y = (y * diag).reshape(pall, 8, width).sum(axis=1)
        pick = (src + b * block_a == dst).astype(F32)
        total += jnp.dot(y, pick, precision=lax.Precision.HIGHEST, preferred_element_type=F32)
    part[...] = total.reshape(no, pairs, block_b * block_a)

    devices = no * nv * na
    me = (occ * nv + vir) * na + aux
    parts[me] = part[occ]

    def final_copy(k):
        j = lax.rem(me + k, devices)
        to = (j // (nv * na), lax.rem(j // na, nv), lax.rem(j, na))
        return pltpu.make_async_remote_copy(
            src_ref=part.at[to[0]],
            dst_ref=parts.at[me],
            send_sem=a_send.at[k],
            recv_sem=a_recv.at[me],
            device_id=to,
            device_id_type=MESH,
        )

    def final_arrival(k):
        j = lax.rem(me + k, devices)
        to = (j // (nv * na), lax.rem(j // na, nv), lax.rem(j, na))
        return pltpu.make_async_remote_copy(
            src_ref=part.at[to[0]],
            dst_ref=parts.at[j],
            send_sem=a_send.at[k],
            recv_sem=a_recv.at[j],
            device_id=to,
            device_id_type=MESH,
        )

    def start_final(k, carry):
        final_copy(k).start()
        return carry

    def wait_final(k, carry):
        final_arrival(k).wait_recv()
        return carry

    def drain_final(k, carry):
        final_copy(k).wait_send()
        return carry

    lax.fori_loop(1, devices, start_final, 0)
    for copy in tau_sends:
        copy.wait_send()

    def drain_right(n, carry):
        for down in (True, False):
            passes = vir > 0 if down else vir < nv - 1

            @pl.when(passes)
            def _():
                right_copy(vir, n, down).wait_send()

            for k in waves:
                u = vir + k if down else vir - k
                here = u < nv if down else u >= 0

                @pl.when(passes & here)
                def _():
                    right_copy(u, n, down).wait_send()
        return carry

    lax.fori_loop(0, nq, drain_right, 0)
    lax.fori_loop(1, devices, wait_final, 0)
    ladder = jnp.sum(parts[...], axis=0)
    for b in range(block_b):
        out[:, b, :] = res[:, b, :] + ladder[:, b * block_a : (b + 1) * block_a]
    lax.fori_loop(1, devices, drain_final, 0)


def local(sizes, amplitudes, pair_mask, left_factor, left_mask, right_factor, right_mask, residual_in):
    no, nv, na = sizes
    pairs, cols, virt = amplitudes.shape
    rows, block_b, auxn = right_factor.shape
    block_a = left_factor.shape[0]
    nq = auxn // QC
    depth = rows * nv
    cq = cols // na
    pall = no * pairs
    ba = block_b * block_a
    vmem = pl.BlockSpec(memory_space=pltpu.VMEM)
    smem = pl.BlockSpec(memory_space=pltpu.SMEM)
    hbm = pl.BlockSpec(memory_space=pltpu.MemorySpace.HBM)
    dma = pltpu.SemaphoreType.DMA
    pieces = min(4, pairs)
    depth2 = CC // 8 * QC
    return pl.pallas_call(
        functools.partial(kernel, no, nv, na),
        out_shape=jax.ShapeDtypeStruct(residual_in.shape, F32),
        in_specs=[smem, smem, smem, hbm, hbm, hbm, vmem],
        out_specs=vmem,
        scratch_shapes=[
            pltpu.VMEM(right_factor.shape, BF16),
            pltpu.VMEM((pairs, cols, virt), BF16),
            pltpu.VMEM(left_factor.shape, BF16),
            pltpu.VMEM((nq, nv, rows, block_b * QC), BF16),
            pltpu.VMEM((no, na, pairs, cq, depth), BF16),
            pltpu.VMEM((max(no - 1, 1), pairs, cq, depth), BF16),
            pltpu.VMEM((2 * block_b * pall * 8, depth2), BF16),
            pltpu.VMEM((block_a * 8, depth2), BF16),
            pltpu.VMEM((2 * block_b * pall * 8, depth2), BF16),
            pltpu.VMEM((block_a * 8, depth2), BF16),
            pltpu.VMEM((2 * block_b * pall * 8, block_a * 8), F32),
            pltpu.VMEM((no, pairs, ba), F32),
            pltpu.VMEM((no * nv * na, pairs, ba), F32),
            dma,
            dma((nq,)),
            dma,
            dma((2, nv, nq)),
            dma((nv, nq)),
            dma((no, 2 * na, pieces)),
            dma((no, na, pieces)),
            dma((no * nv * na,)),
            dma((no * nv * na,)),
            pltpu.SemaphoreType.REGULAR((2,)),
        ],
        compiler_params=pltpu.CompilerParams(
            collective_id=0, has_side_effects=True, vmem_limit_bytes=62 * 1024 * 1024
        ),
        name="ladder",
    )(pair_mask, left_mask, right_mask, amplitudes, left_factor, right_factor, residual_in)


def solution(mesh):
    sizes = tuple(mesh.shape[name] for name in ("occ", "vir", "aux"))
    return jax.shard_map(
        functools.partial(local, sizes),
        mesh=mesh,
        in_specs=(
            P("occ", "vir", None),
            P("occ", "vir", None),
            P(None, "vir", "aux"),
            P("vir", "aux"),
            P(("occ", "vir"), None, "aux"),
            P(None, "aux"),
            P("occ", None, None),
        ),
        out_specs=P("occ", None, None),
        check_vma=False,
    )
```

time: 119 us -> 96.8 us (0.81)
  Pallas kernels: 113 us -> 95.2 us
  local copies, waits for them, and re-layouts: 5.9 us -> 1.32 us
    pallas_call x1, Pallas kernels: 113 us -> 95.2 us  [local(): pl.pallas_call(functools.partial(kernel, no, nv, na), out_shape=jax.Shape...]
    reshape x4 -> x0, local copies, waits for them, and re-layouts: 5.9 us -> none  [the longest x1 1.59 us: local(): right = right_factor.reshape(rows, block_b, nq, QC).transpose(2, 0, 1, 3)]
    unnamed x0 -> x1, local copies, waits for them, and re-layouts: none -> 1.32 us
where the time goes in v1:
time: 96.8 us; the launch traced here: 96.5 us
  Pallas kernels  95.2 us (98%)
  local copies, waits for them, and re-layouts  1.32 us (1%)
    pallas_call x1, Pallas kernels, local(): pl.pallas_call(functools.partial(kernel, no, nv, na), out_shape=jax.Shape...  95.2 us

profile of v1, /device:TPU:0, one launch (start us, length us, event | category | flops | bytes accessed | tf_op | source)
XLA Modules:
  0.0 96.5 jit_solution(7343317802306807237)
XLA Ops:
  0.0 95.2 %ladder.1 = f32[8,4,32]{2,1,0:T(4,128)} custom-call(s32[8,2,8]{2,1,0:T(2,128)} %pair_mask.1, s32[2,8]{1,0:T(2,128)} %left_mask.1, s32[8,8]{1,0:T(8,128)} %right_mask.1, bf16[8,256,1024]{2,1,0:T(8,128)(2,1)} %amp_hbm.1, bf16[32,256,1024]{2,1,0:T(8,128)(2,1)} %left_hbm.1, bf16[128,4,1024]{2,1,0:T(4,128)(2,1)} %right_hbm.1, f32[8,4,32]{2,1,0:T(4,128)} %res.1), custom_call_target="tpu_custom_call" | custom-call | tf_op jit(solution)/shard_map/ladder/pallas_call | solution.py:407
  95.2 1.3 %copy.9 = f32[8,4,32]{2,1,0:T(4,128)} copy(f32[8,4,32]{2,1,0:T(4,128)} %ladder.1) | data formatting | bytes 8192

commit v2 on v1

--- a/solution.py
+++ b/solution.py
@@ -9,33 +9,37 @@
 
 TILE = 128
 QC = 128
-CC = 32
-AHEAD = 4
+CC = 64
+BB = 2
+AHEAD = 6
 MESH = pl.DeviceIdType.MESH
 F32 = jnp.float32
 BF16 = jnp.bfloat16
 
 
 def kernel(
-    no, nv, na, pair_mask, left_mask, right_mask, amp_hbm, left_hbm, right_hbm, res,
-    out, raw, amp, left, rbuf, tau, tsend, lhs_a, rhs_a, lhs_b, rhs_b, acc, part, parts,
-    amp_sem, left_sem, raw_sem, r_send, r_recv, t_send, t_recv, a_send, a_recv, enter,
+    no, nv, na, pair_hbm, lmask_hbm, rmask_hbm, amp_hbm, left_hbm, right_hbm, res_hbm,
+    out, pair_mask, left_mask, right_mask, res, pick, raw, amp, left, rbuf, tau, tsend, rhs, lhs_a, lhs_b, acc, part, parts,
+    small_sem, amp_sem, left_sem, raw_sem, r_send, r_recv, t_send, t_recv, a_send, a_recv, enter,
 ):
     occ, vir, aux = lax.axis_index("occ"), lax.axis_index("vir"), lax.axis_index("aux")
     pairs, cols, virt = amp.shape
-    nq, _, rows, bq = rbuf.shape
-    block_b = bq // QC
+    nch, _, rows, bq = rbuf.shape
+    block_b = raw.shape[1]
+    nbp = block_b // BB
+    nq = nch // nbp
     block_a = left.shape[0]
     cq, depth = tau.shape[3], tau.shape[4]
     pall = no * pairs
-    steps = cols // CC
-    subs = cq // CC
-    groups = CC // 8
+    cc = min(CC, cq)
+    steps = cols // cc
+    subs = cq // cc
+    groups = cc // 8
     half = pall * 8
     pieces = min(4, pairs)
     pp = pairs // pieces
     waves = list(range(1, nv))
-    lead = max(3, nv - 2)
+    lead = max(6, nv - 2)
 
     place = {"occ": (occ, no), "vir": (vir, nv), "aux": (aux, na)}
 
@@ -50,11 +54,43 @@
                 count += 1
         return count
 
-    greeted = greet(pltpu.get_barrier_semaphore(), ("occ", "vir", "aux"))
+    def reach(sem, d):
+        for ok, to in ((vir >= d, vir - d), (vir + d < nv, vir + d)):
+            @pl.when(ok)
+            def _():
+                pl.semaphore_signal(sem, inc=1, device_id={"vir": to}, device_id_type=MESH)
+        return (vir >= d).astype(jnp.int32) + (vir + d < nv).astype(jnp.int32)
+
+    barrier = pltpu.get_barrier_semaphore()
+    greeted = greet(barrier, ("occ", "aux")) + reach(barrier, 1)
+    spans = [1 << i for i in range((nv - 1).bit_length())]
+    rounds = [functools.partial(reach, d=d) for d in spans]
+    rounds.append(functools.partial(greet, axes=("aux",)))
+    owed = []
+
+    def next_round():
+        i = len(owed)
+        if i:
+            pl.semaphore_wait(enter.at[i - 1], owed[i - 1])
+        if i < len(rounds):
+            owed.append(rounds[i](enter.at[i]))
+        elif i == len(rounds):
+            owed.append(None)
+
+    smalls = [
+        pltpu.make_async_copy(*pair, small_sem.at[i])
+        for i, pair in enumerate(
+            ((rmask_hbm, right_mask), (pair_hbm, pair_mask), (lmask_hbm, left_mask), (res_hbm, res))
+        )
+    ]
+    for copy in smalls[:2]:
+        copy.start()
     raw_copy = pltpu.make_async_copy(right_hbm, raw, raw_sem)
     raw_copy.start()
     amp_copy = pltpu.make_async_copy(amp_hbm, amp, amp_sem)
     amp_copy.start()
+    for copy in smalls[2:]:
+        copy.start()
 
     def right_copy(u, n, down):
         return pltpu.make_async_remote_copy(
@@ -91,18 +127,18 @@
         n = m - k + 1
         if k <= nv - 2:
             if isinstance(m, int):
-                if 0 <= n < nq:
+                if 0 <= n < nch:
                     arrive(k, n, True)
             else:
-                arrive(k, n, True, (n >= 0) & (n < nq))
+                arrive(k, n, True, (n >= 0) & (n < nch))
 
     def more_own(m):
         n = m + AHEAD
         if isinstance(m, int):
-            if n < nq:
+            if n < nch:
                 send_own(n)
         else:
-            @pl.when(n < nq)
+            @pl.when(n < nch)
             def _():
                 send_own(n)
 
@@ -127,11 +163,14 @@
             m = right_mask[(first + r) // TILE, n * QC // TILE].astype(F32)
             x = raw[pl.ds(r, sub_rows), :, pl.ds(pl.multiple_of(n * QC, QC), QC)].astype(F32) * m
             for b in range(block_b):
-                rbuf[n, vir, r : r + sub_rows, b * QC : (b + 1) * QC] = x[:, b, :].astype(BF16)
-        return carry
-
+                j, e = n * nbp + b // BB, b % BB
+                rbuf[j, vir, r : r + sub_rows, e * QC : (e + 1) * QC] = x[:, b, :].astype(BF16)
+        return carry
+
+    smalls[0].wait()
     raw_copy.wait()
     lax.fori_loop(0, nq, arrange, 0)
+    smalls[1].wait()
     amp_copy.wait()
     for n in range(nq):
         left_copy(n).start()
@@ -178,8 +217,8 @@
         )
 
     lax.fori_loop(0, pairs, fill_send, 0)
-    pl.semaphore_wait(pltpu.get_barrier_semaphore(), greeted)
-    for n in range(min(AHEAD, nq)):
+    pl.semaphore_wait(barrier, greeted)
+    for n in range(min(AHEAD, nch)):
         send_own(n)
     tau_sends = []
     for h in range(pieces):
@@ -187,10 +226,15 @@
             copy = occ_copy(k, h)
             copy.start()
             tau_sends.append(copy)
-
+    next_round()
+
+    ba = block_b * block_a
+    wide = block_b * block_a * 8
+    src = lax.broadcasted_iota(jnp.int32, (wide, ba), 0) // 8
+    dst = lax.broadcasted_iota(jnp.int32, (wide, ba), 1)
+    pick[...] = (src == dst).astype(F32).astype(BF16)
     acc[...] = jnp.zeros_like(acc)
     lhs_b[...] = jnp.zeros_like(lhs_b)
-    rhs_b[...] = jnp.zeros_like(rhs_b)
 
     def fill_own(i, carry):
         p, q = i // na, lax.rem(i, na)
@@ -230,6 +274,24 @@
                     copy.start()
                     tau_sends.append(copy)
 
+    def prepare(i, carry):
+        n, cs = i // steps, lax.rem(i, steps)
+
+        @pl.when(cs == 0)
+        def _():
+            left_copy(n).wait()
+
+        c0 = pl.multiple_of(cs * cc, cc)
+        q0 = pl.multiple_of(n * QC, QC)
+        lm = left_mask[cs * cc // TILE, n * QC // TILE].astype(F32)
+        w = left[:, pl.ds(c0, cc), pl.ds(q0, QC)].astype(F32) * lm
+        w = w.reshape(block_a, groups, 8, QC)
+        for j in range(groups):
+            rhs[i, :, j * QC : (j + 1) * QC] = w[:, j].reshape(block_a * 8, QC).astype(BF16)
+        return carry
+
+    smalls[2].wait()
+    ready = 0
     done = 0
     for w in range(pieces + len(bits)):
         for s in range(len(news)):
@@ -238,86 +300,81 @@
         while done < lead and (done + 1) * (pieces + len(bits)) <= (w + 1) * lead:
             slot(done)
             done += 1
+        if 0 < w <= len(rounds):
+            next_round()
+        upto = nq * steps * (w + 1) // (pieces + len(bits))
+        lax.fori_loop(ready, upto, prepare, 0)
+        ready = upto
     while done < lead:
         slot(done)
         done += 1
-    pl.semaphore_wait(enter.at[0], greet(enter.at[0], ("vir",)))
-    pl.semaphore_wait(enter.at[1], greet(enter.at[1], ("aux",)))
-
-    def stage_two(lhs, rhs):
-        acc[...] += lax.dot_general(
-            lhs[...], rhs[...], (((1,), (1,)), ((), ())), preferred_element_type=F32
-        )
-
-    def stage_one(n, cs, lhs, rhs):
-        c0 = pl.multiple_of(cs * CC, CC)
-        q0 = pl.multiple_of(n * QC, QC)
-        lm = left_mask[cs * CC // TILE, n * QC // TILE].astype(F32)
-        w = left[:, pl.ds(c0, CC), pl.ds(q0, QC)].astype(F32) * lm
-        w = w.reshape(block_a, groups, 8, QC)
+    while len(owed) <= len(rounds):
+        next_round()
+    lax.fori_loop(ready, nq * steps, prepare, 0)
+
+    def stage_two(e, lhs, i):
+        span = pl.ds(pl.multiple_of(e * (2 * BB * half), 2 * BB * half), 2 * BB * half)
+        acc[span, :] += lax.dot_general(
+            lhs[...], rhs[i], (((1,), (1,)), ((), ())), preferred_element_type=F32
+        )
+
+    def stage_one(ch, cs, lhs):
+        q, s = cs // subs, lax.rem(cs, subs)
+        t = tau[:, q, :, pl.ds(pl.multiple_of(s * cc, cc), cc), :].reshape(pall * cc, depth)
+        r = rbuf[ch].reshape(depth, bq)
+        inner = jnp.dot(t, r, preferred_element_type=F32)
+        inner = inner.reshape(pall, groups, 8, bq)
         for j in range(groups):
-            rhs[:, j * QC : (j + 1) * QC] = w[:, j].reshape(block_a * 8, QC).astype(BF16)
-        q, s = cs // subs, lax.rem(cs, subs)
-        t = tau[:, q, :, pl.ds(pl.multiple_of(s * CC, CC), CC), :].reshape(pall * CC, depth)
-        for b in range(0, block_b, 2):
-            r = rbuf[n, :, :, b * QC : (b + 2) * QC].reshape(depth, 2 * QC)
-            inner = jnp.dot(t, r, preferred_element_type=F32)
-            inner = inner.reshape(pall, groups, 8, 2 * QC)
-            for j in range(groups):
-                for e in range(2):
-                    x = inner[:, j, :, e * QC : (e + 1) * QC].reshape(half, QC)
-                    hi = x.astype(BF16)
-                    lo = (x - hi.astype(F32)).astype(BF16)
-                    row = 2 * (b + e) * half
-                    lhs[row : row + half, j * QC : (j + 1) * QC] = hi
-                    lhs[row + half : row + 2 * half, j * QC : (j + 1) * QC] = lo
+            for e in range(BB):
+                x = inner[:, j, :, e * QC : (e + 1) * QC].reshape(half, QC)
+                hi = x.astype(BF16)
+                lo = (x - hi.astype(F32)).astype(BF16)
+                row = 2 * e * half
+                lhs[row : row + half, j * QC : (j + 1) * QC] = hi
+                lhs[row + half : row + 2 * half, j * QC : (j + 1) * QC] = lo
 
     turns = steps // 2
 
     def turn(it, carry):
-        n = it // turns
+        ch = it // turns
         ds = lax.rem(it, turns)
+        n, e = ch // nbp, lax.rem(ch, nbp)
 
         @pl.when(ds == 0)
         def _():
             for k in waves:
-                arrive(k, n, False)
-            left_copy(n).wait()
-
-        for k in waves[:-1]:
-            @pl.when(ds == min(k, turns - 1))
-            def _():
-                relay(k, n + lead)
-                if k == 1:
-                    more_own(n + lead)
-
-        if nv <= 2:
-            @pl.when(ds == 0)
-            def _():
-                more_own(n + lead)
-
-        stage_two(lhs_b, rhs_b)
-        stage_one(n, 2 * ds, lhs_a, rhs_a)
-        stage_two(lhs_a, rhs_a)
-        stage_one(n, 2 * ds + 1, lhs_b, rhs_b)
-        return carry
-
-    lax.fori_loop(0, nq * turns, turn, 0)
-    stage_two(lhs_b, rhs_b)
+                arrive(k, ch, False)
+
+        @pl.when(ds == turns - 1)
+        def _():
+            slot(ch + lead)
+
+        last = jnp.maximum(it - 1, 0) // turns
+        back = jnp.where(ds == 0, last // nbp * steps + steps - 1, n * steps + 2 * ds - 1)
+        stage_one(ch, 2 * ds, lhs_a)
+        stage_two(lax.rem(last, nbp), lhs_b, back)
+        stage_one(ch, 2 * ds + 1, lhs_b)
+        stage_two(e, lhs_a, n * steps + 2 * ds)
+        return carry
+
+    lax.fori_loop(0, nch * turns, turn, 0)
+    stage_two(nbp - 1, lhs_b, nq * steps - 1)
 
     width = block_a * 8
     row_i = lax.rem(lax.broadcasted_iota(jnp.int32, (half, width), 0), 8)
     col_i = lax.rem(lax.broadcasted_iota(jnp.int32, (half, width), 1), 8)
     diag = (row_i == col_i).astype(F32)
-    total = jnp.zeros((pall, block_b * block_a), F32)
-    src = lax.broadcasted_iota(jnp.int32, (width, block_b * block_a), 0) // 8
-    dst = lax.broadcasted_iota(jnp.int32, (width, block_b * block_a), 1)
+    total = jnp.zeros((pall, ba), F32)
     for b in range(block_b):
         y = acc[2 * b * half : (2 * b + 1) * half, :] + acc[(2 * b + 1) * half : (2 * b + 2) * half, :]
         y = (y * diag).reshape(pall, 8, width).sum(axis=1)
-        pick = (src + b * block_a == dst).astype(F32)
-        total += jnp.dot(y, pick, precision=lax.Precision.HIGHEST, preferred_element_type=F32)
-    part[...] = total.reshape(no, pairs, block_b * block_a)
+        for _ in range(3):
+            z = y.astype(BF16)
+            total += jnp.dot(
+                z, pick[b * width : (b + 1) * width, :], preferred_element_type=F32
+            )
+            y = y - z.astype(F32)
+    part[...] = total.reshape(no, pairs, ba)
 
     devices = no * nv * na
     me = (occ * nv + vir) * na + aux
@@ -380,8 +437,9 @@
                     right_copy(u, n, down).wait_send()
         return carry
 
-    lax.fori_loop(0, nq, drain_right, 0)
+    lax.fori_loop(0, nch, drain_right, 0)
     lax.fori_loop(1, devices, wait_final, 0)
+    smalls[3].wait()
     ladder = jnp.sum(parts[...], axis=0)
     for b in range(block_b):
         out[:, b, :] = res[:, b, :] + ladder[:, b * block_a : (b + 1) * block_a]
@@ -394,45 +452,50 @@
     rows, block_b, auxn = right_factor.shape
     block_a = left_factor.shape[0]
     nq = auxn // QC
+    nch = nq * block_b // BB
     depth = rows * nv
     cq = cols // na
     pall = no * pairs
     ba = block_b * block_a
     vmem = pl.BlockSpec(memory_space=pltpu.VMEM)
-    smem = pl.BlockSpec(memory_space=pltpu.SMEM)
     hbm = pl.BlockSpec(memory_space=pltpu.MemorySpace.HBM)
     dma = pltpu.SemaphoreType.DMA
     pieces = min(4, pairs)
-    depth2 = CC // 8 * QC
+    inner = min(CC, cq) // 8 * QC
     return pl.pallas_call(
         functools.partial(kernel, no, nv, na),
         out_shape=jax.ShapeDtypeStruct(residual_in.shape, F32),
-        in_specs=[smem, smem, smem, hbm, hbm, hbm, vmem],
+        in_specs=[hbm] * 7,
         out_specs=vmem,
         scratch_shapes=[
+            pltpu.SMEM(pair_mask.shape, jnp.int32),
+            pltpu.SMEM(left_mask.shape, jnp.int32),
+            pltpu.SMEM(right_mask.shape, jnp.int32),
+            pltpu.VMEM(residual_in.shape, F32),
+            pltpu.VMEM((ba * 8, ba), BF16),
             pltpu.VMEM(right_factor.shape, BF16),
             pltpu.VMEM((pairs, cols, virt), BF16),
             pltpu.VMEM(left_factor.shape, BF16),
-            pltpu.VMEM((nq, nv, rows, block_b * QC), BF16),
+            pltpu.VMEM((nch, nv, rows, BB * QC), BF16),
             pltpu.VMEM((no, na, pairs, cq, depth), BF16),
             pltpu.VMEM((max(no - 1, 1), pairs, cq, depth), BF16),
-            pltpu.VMEM((2 * block_b * pall * 8, depth2), BF16),
-            pltpu.VMEM((block_a * 8, depth2), BF16),
-            pltpu.VMEM((2 * block_b * pall * 8, depth2), BF16),
-            pltpu.VMEM((block_a * 8, depth2), BF16),
+            pltpu.VMEM((nq * cols // min(CC, cq), block_a * 8, inner), BF16),
+            pltpu.VMEM((2 * BB * pall * 8, inner), BF16),
+            pltpu.VMEM((2 * BB * pall * 8, inner), BF16),
             pltpu.VMEM((2 * block_b * pall * 8, block_a * 8), F32),
             pltpu.VMEM((no, pairs, ba), F32),
             pltpu.VMEM((no * nv * na, pairs, ba), F32),
+            dma((4,)),
             dma,
             dma((nq,)),
             dma,
-            dma((2, nv, nq)),
-            dma((nv, nq)),
+            dma((2, nv, nch)),
+            dma((nv, nch)),
             dma((no, 2 * na, pieces)),
             dma((no, na, pieces)),
             dma((no * nv * na,)),
             dma((no * nv * na,)),
-            pltpu.SemaphoreType.REGULAR((2,)),
+            pltpu.SemaphoreType.REGULAR((nv.bit_length() + 1,)),
         ],
         compiler_params=pltpu.CompilerParams(
             collective_id=0, has_side_effects=True, vmem_limit_bytes=62 * 1024 * 1024

time: 96.8 us -> 92.1 us (0.951)
  Pallas kernels: 95.2 us -> 90.5 us
    pallas_call x1, Pallas kernels: 95.2 us -> 90.5 us  [local(): pl.pallas_call(functools.partial(kernel, no, nv, na), out_shape=jax.Shape...]
where the time goes in v2:
time: 92.1 us; the launch traced here: 91.8 us
  Pallas kernels  90.5 us (98%)
  local copies, waits for them, and re-layouts  1.32 us (1%)
    pallas_call x1, Pallas kernels, local(): pl.pallas_call(functools.partial(kernel, no, nv, na), out_shape=jax.Shape...  90.5 us

profile of v2, /device:TPU:0, one launch (start us, length us, event | category | flops | bytes accessed | tf_op | source)
XLA Modules:
  0.0 91.8 jit_solution(12690175705230839948)
XLA Ops:
  0.0 90.5 %ladder.1 = f32[8,4,32]{2,1,0:T(4,128)} custom-call(s32[8,2,8]{2,1,0:T(2,128)} %pair_hbm.1, s32[2,8]{1,0:T(2,128)} %lmask_hbm.1, s32[8,8]{1,0:T(8,128)} %rmask_hbm.1, bf16[8,256,1024]{2,1,0:T(8,128)(2,1)} %amp_hbm.1, bf16[32,256,1024]{2,1,0:T(8,128)(2,1)} %left_hbm.1, bf16[128,4,1024]{2,1,0:T(4,128)(2,1)} %right_hbm.1, f32[8,4,32]{2,1,0:T(4,128)} %res_hbm.1), custom_call_target="tpu_custom_call" | custom-call | tf_op jit(solution)/shard_map/ladder/pallas_call | solution.py:465
  90.5 1.3 %copy.9 = f32[8,4,32]{2,1,0:T(4,128)} copy(f32[8,4,32]{2,1,0:T(4,128)} %ladder.1) | data formatting | bytes 8192

commit v3 on v2

--- a/solution.py
+++ b/solution.py
@@ -11,7 +11,7 @@
 QC = 128
 CC = 64
 BB = 2
-AHEAD = 6
+AHEAD = 4
 MESH = pl.DeviceIdType.MESH
 F32 = jnp.float32
 BF16 = jnp.bfloat16
@@ -24,10 +24,10 @@
 ):
     occ, vir, aux = lax.axis_index("occ"), lax.axis_index("vir"), lax.axis_index("aux")
     pairs, cols, virt = amp.shape
-    nch, _, rows, bq = rbuf.shape
+    nq, _, nbp, rows, bq = rbuf.shape
     block_b = raw.shape[1]
-    nbp = block_b // BB
-    nq = nch // nbp
+    nch = nq * nbp
+    units = nq - 1 + nbp
     block_a = left.shape[0]
     cq, depth = tau.shape[3], tau.shape[4]
     pall = no * pairs
@@ -39,7 +39,7 @@
     pieces = min(4, pairs)
     pp = pairs // pieces
     waves = list(range(1, nv))
-    lead = max(6, nv - 2)
+    lead = max(3, nv - 2)
 
     place = {"occ": (occ, no), "vir": (vir, nv), "aux": (aux, na)}
 
@@ -92,61 +92,70 @@
     for copy in smalls[2:]:
         copy.start()
 
-    def right_copy(u, n, down):
+    def right_copy(u, m, down, big):
+        block = rbuf.at[m, u] if big else rbuf.at[nq - 1, u, m - (nq - 1)]
         return pltpu.make_async_remote_copy(
-            src_ref=rbuf.at[n, u],
-            dst_ref=rbuf.at[n, u],
-            send_sem=r_send.at[1 if down else 0, u, n],
-            recv_sem=r_recv.at[u, n],
+            src_ref=block,
+            dst_ref=block,
+            send_sem=r_send.at[1 if down else 0, u, m],
+            recv_sem=r_recv.at[u, m],
             device_id={"vir": vir - 1 if down else vir + 1},
             device_id_type=MESH,
         )
 
-    def send_own(n):
-        @pl.when(vir > 0)
+    def sized(m, act, ok=True):
+        if isinstance(m, int):
+            if 0 <= m < units:
+                act(m < nq - 1)
+            return
+
+        @pl.when(ok & (m >= 0) & (m < nq - 1))
         def _():
-            right_copy(vir, n, True).start()
-
-        @pl.when(vir < nv - 1)
+            act(True)
+
+        @pl.when(ok & (m >= nq - 1) & (m < units))
         def _():
-            right_copy(vir, n, False).start()
-
-    def arrive(k, n, forwarded, valid=True):
-        for down in (True, False):
-            u = vir + k if down else vir - k
-            here = u < nv if down else u >= 0
-            passes = vir > 0 if down else vir < nv - 1
-
-            @pl.when(here & (passes if forwarded else jnp.logical_not(passes)) & valid)
+            act(False)
+
+    def send_own(m):
+        def act(big):
+            @pl.when(vir > 0)
             def _():
-                right_copy(u, n, down).wait_recv()
-                if forwarded:
-                    right_copy(u, n, down).start()
-
-    def relay(k, m):
-        n = m - k + 1
-        if k <= nv - 2:
-            if isinstance(m, int):
-                if 0 <= n < nch:
-                    arrive(k, n, True)
-            else:
-                arrive(k, n, True, (n >= 0) & (n < nch))
-
-    def more_own(m):
-        n = m + AHEAD
+                right_copy(vir, m, True, big).start()
+
+            @pl.when(vir < nv - 1)
+            def _():
+                right_copy(vir, m, False, big).start()
+
+        sized(m, act)
+
+    def arrive(k, m, forwarded, ok=True):
+        def act(big):
+            for down in (True, False):
+                u = vir + k if down else vir - k
+                here = u < nv if down else u >= 0
+                passes = vir > 0 if down else vir < nv - 1
+
+                @pl.when(here & (passes if forwarded else jnp.logical_not(passes)))
+                def _():
+                    right_copy(u, m, down, big).wait_recv()
+                    if forwarded:
+                        right_copy(u, m, down, big).start()
+
+        sized(m, act, ok)
+
+    def slot(m):
+        for k in reversed(waves[:-1]):
+            arrive(k, m - k + 1, True, (vir > 0) & (vir < nv - 1))
         if isinstance(m, int):
-            if n < nch:
-                send_own(n)
+            if m == 0:
+                send_own(AHEAD)
+            elif m % 2:
+                send_own(AHEAD + (m + 1) // 2)
         else:
-            @pl.when(n < nch)
+            @pl.when(lax.rem(m, 2) == 1)
             def _():
-                send_own(n)
-
-    def slot(m):
-        relay(1, m)
-        more_own(m)
-        for k in waves[1:]:
-            relay(k, m)
+                send_own(AHEAD + (m + 1) // 2)
 
     def left_copy(n):
         return pltpu.make_async_copy(
@@ -163,8 +172,10 @@
             m = right_mask[(first + r) // TILE, n * QC // TILE].astype(F32)
             x = raw[pl.ds(r, sub_rows), :, pl.ds(pl.multiple_of(n * QC, QC), QC)].astype(F32) * m
             for b in range(block_b):
-                j, e = n * nbp + b // BB, b % BB
-                rbuf[j, vir, r : r + sub_rows, e * QC : (e + 1) * QC] = x[:, b, :].astype(BF16)
+                e = b % BB
+                rbuf[n, vir, b // BB, r : r + sub_rows, e * QC : (e + 1) * QC] = x[:, b, :].astype(
+                    BF16
+                )
         return carry
 
     smalls[0].wait()
@@ -218,7 +229,7 @@
 
     lax.fori_loop(0, pairs, fill_send, 0)
     pl.semaphore_wait(barrier, greeted)
-    for n in range(min(AHEAD, nch)):
+    for n in range(AHEAD):
         send_own(n)
     tau_sends = []
     for h in range(pieces):
@@ -318,10 +329,10 @@
             lhs[...], rhs[i], (((1,), (1,)), ((), ())), preferred_element_type=F32
         )
 
-    def stage_one(ch, cs, lhs):
+    def stage_one(n, e, cs, lhs):
         q, s = cs // subs, lax.rem(cs, subs)
         t = tau[:, q, :, pl.ds(pl.multiple_of(s * cc, cc), cc), :].reshape(pall * cc, depth)
-        r = rbuf[ch].reshape(depth, bq)
+        r = rbuf[n, :, e].reshape(depth, bq)
         inner = jnp.dot(t, r, preferred_element_type=F32)
         inner = inner.reshape(pall, groups, 8, bq)
         for j in range(groups):
@@ -333,31 +344,31 @@
                 lhs[row : row + half, j * QC : (j + 1) * QC] = hi
                 lhs[row + half : row + 2 * half, j * QC : (j + 1) * QC] = lo
 
-    turns = steps // 2
-
-    def turn(it, carry):
-        ch = it // turns
-        ds = lax.rem(it, turns)
+    def chunk(ch, carry):
         n, e = ch // nbp, lax.rem(ch, nbp)
-
-        @pl.when(ds == 0)
+        ending = n == nq - 1
+        unit = jnp.where(ending, nq - 1 + e, n)
+
+        @pl.when(ending | (e == 0))
         def _():
             for k in waves:
-                arrive(k, ch, False)
-
-        @pl.when(ds == turns - 1)
+                arrive(k, unit, False)
+
+        @pl.when((ending | (e == nbp - 1)) & (unit + lead < units + nv - 3))
         def _():
-            slot(ch + lead)
-
-        last = jnp.maximum(it - 1, 0) // turns
-        back = jnp.where(ds == 0, last // nbp * steps + steps - 1, n * steps + 2 * ds - 1)
-        stage_one(ch, 2 * ds, lhs_a)
-        stage_two(lax.rem(last, nbp), lhs_b, back)
-        stage_one(ch, 2 * ds + 1, lhs_b)
-        stage_two(e, lhs_a, n * steps + 2 * ds)
-        return carry
-
-    lax.fori_loop(0, nch * turns, turn, 0)
+            slot(unit + lead)
+
+        last = jnp.maximum(ch - 1, 0)
+        for cs in range(steps):
+            now, old = (lhs_a, lhs_b) if cs % 2 == 0 else (lhs_b, lhs_a)
+            stage_one(n, e, cs, now)
+            if cs == 0:
+                stage_two(lax.rem(last, nbp), old, last // nbp * steps + steps - 1)
+            else:
+                stage_two(e, old, n * steps + cs - 1)
+        return carry
+
+    lax.fori_loop(0, nch, chunk, 0)
     stage_two(nbp - 1, lhs_b, nq * steps - 1)
 
     width = block_a * 8
@@ -420,24 +431,27 @@
     for copy in tau_sends:
         copy.wait_send()
 
-    def drain_right(n, carry):
-        for down in (True, False):
-            passes = vir > 0 if down else vir < nv - 1
-
-            @pl.when(passes)
-            def _():
-                right_copy(vir, n, down).wait_send()
-
-            for k in waves:
-                u = vir + k if down else vir - k
-                here = u < nv if down else u >= 0
-
-                @pl.when(passes & here)
+    def drain_right(m, carry):
+        def act(big):
+            for down in (True, False):
+                passes = vir > 0 if down else vir < nv - 1
+
+                @pl.when(passes)
                 def _():
-                    right_copy(u, n, down).wait_send()
-        return carry
-
-    lax.fori_loop(0, nch, drain_right, 0)
+                    right_copy(vir, m, down, big).wait_send()
+
+                for k in waves:
+                    u = vir + k if down else vir - k
+                    here = u < nv if down else u >= 0
+
+                    @pl.when(passes & here)
+                    def _():
+                        right_copy(u, m, down, big).wait_send()
+
+        sized(m, act)
+        return carry
+
+    lax.fori_loop(0, units, drain_right, 0)
     lax.fori_loop(1, devices, wait_final, 0)
     smalls[3].wait()
     ladder = jnp.sum(parts[...], axis=0)
@@ -452,7 +466,7 @@
     rows, block_b, auxn = right_factor.shape
     block_a = left_factor.shape[0]
     nq = auxn // QC
-    nch = nq * block_b // BB
+    units = nq - 1 + block_b // BB
     depth = rows * nv
     cq = cols // na
     pall = no * pairs
@@ -476,7 +490,7 @@
             pltpu.VMEM(right_factor.shape, BF16),
             pltpu.VMEM((pairs, cols, virt), BF16),
             pltpu.VMEM(left_factor.shape, BF16),
-            pltpu.VMEM((nch, nv, rows, BB * QC), BF16),
+            pltpu.VMEM((nq, nv, block_b // BB, rows, BB * QC), BF16),
             pltpu.VMEM((no, na, pairs, cq, depth), BF16),
             pltpu.VMEM((max(no - 1, 1), pairs, cq, depth), BF16),
             pltpu.VMEM((nq * cols // min(CC, cq), block_a * 8, inner), BF16),
@@ -489,8 +503,8 @@
             dma,
             dma((nq,)),
             dma,
-            dma((2, nv, nch)),
-            dma((nv, nch)),
+            dma((2, nv, units)),
+            dma((nv, units)),
             dma((no, 2 * na, pieces)),
             dma((no, na, pieces)),
             dma((no * nv * na,)),

time: 92.1 us -> 90.2 us (0.979)
  Pallas kernels: 90.5 us -> 88.6 us
    pallas_call x1, Pallas kernels: 90.5 us -> 88.6 us  [local(): pl.pallas_call(functools.partial(kernel, no, nv, na), out_shape=jax.Shape...]
where the time goes in v3:
time: 90.2 us; the launch traced here: 90 us
  Pallas kernels  88.6 us (98%)
  local copies, waits for them, and re-layouts  1.32 us (1%)
    pallas_call x1, Pallas kernels, local(): pl.pallas_call(functools.partial(kernel, no, nv, na), out_shape=jax.Shape...  88.6 us

profile of v3, /device:TPU:0, one launch (start us, length us, event | category | flops | bytes accessed | tf_op | source)
XLA Modules:
  0.0 90.0 jit_solution(15823993428765233153)
XLA Ops:
  0.0 88.6 %ladder.1 = f32[8,4,32]{2,1,0:T(4,128)} custom-call(s32[8,2,8]{2,1,0:T(2,128)} %pair_hbm.1, s32[2,8]{1,0:T(2,128)} %lmask_hbm.1, s32[8,8]{1,0:T(8,128)} %rmask_hbm.1, bf16[8,256,1024]{2,1,0:T(8,128)(2,1)} %amp_hbm.1, bf16[32,256,1024]{2,1,0:T(8,128)(2,1)} %left_hbm.1, bf16[128,4,1024]{2,1,0:T(4,128)(2,1)} %right_hbm.1, f32[8,4,32]{2,1,0:T(4,128)} %res_hbm.1), custom_call_target="tpu_custom_call" | custom-call | tf_op jit(solution)/shard_map/ladder/pallas_call | solution.py:479
  88.6 1.3 %copy.9 = f32[8,4,32]{2,1,0:T(4,128)} copy(f32[8,4,32]{2,1,0:T(4,128)} %ladder.1) | data formatting | bytes 8192

commit v4 on v3

--- a/solution.py
+++ b/solution.py
@@ -150,12 +150,19 @@
         if isinstance(m, int):
             if m == 0:
                 send_own(AHEAD)
+            elif m >= 2 * AHEAD:
+                send_own(m + 1)
             elif m % 2:
                 send_own(AHEAD + (m + 1) // 2)
         else:
-            @pl.when(lax.rem(m, 2) == 1)
+            @pl.when((lax.rem(m, 2) == 1) & (m < 2 * AHEAD))
             def _():
                 send_own(AHEAD + (m + 1) // 2)
+
+            if units > 2 * AHEAD + 1:
+                @pl.when(m >= 2 * AHEAD)
+                def _():
+                    send_own(m + 1)
 
     def left_copy(n):
         return pltpu.make_async_copy(
@@ -478,7 +485,7 @@
     inner = min(CC, cq) // 8 * QC
     return pl.pallas_call(
         functools.partial(kernel, no, nv, na),
-        out_shape=jax.ShapeDtypeStruct(residual_in.shape, F32),
+        out_shape=pltpu.VMEM(residual_in.shape, F32),
         in_specs=[hbm] * 7,
         out_specs=vmem,
         scratch_shapes=[

time: 90.2 us -> 88.8 us (0.984)
  no operation moved by 1% of the time
where the time goes in v4:
time: 88.8 us; the launch traced here: 88.6 us
  Pallas kernels  88 us (99%)
    pallas_call x1, Pallas kernels, local(): pl.pallas_call(functools.partial(kernel, no, nv, na), out_shape=pltpu.VME...  88 us

profile of v4, /device:TPU:0, one launch (start us, length us, event | category | flops | bytes accessed | tf_op | source)
XLA Modules:
  0.0 88.6 jit_solution(18359905379762159289)
XLA Ops:
  0.0 88.0 %ladder.1 = f32[8,4,32]{2,1,0:T(4,128)S(1)} custom-call(s32[8,2,8]{2,1,0:T(2,128)} %pair_hbm.1, s32[2,8]{1,0:T(2,128)} %lmask_hbm.1, s32[8,8]{1,0:T(8,128)} %rmask_hbm.1, bf16[8,256,1024]{2,1,0:T(8,128)(2,1)} %amp_hbm.1, bf16[32,256,1024]{2,1,0:T(8,128)(2,1)} %left_hbm.1, bf16[128,4,1024]{2,1,0:T(4,128)(2,1)} %right_hbm.1, f32[8,4,32]{2,1,0:T(4,128)} %res_hbm.1), custom_call_target="tpu_custom_call" | custom-call | tf_op jit(solution)/shard_map/ladder/pallas_call | solution.py:486
  88.0 0.6 copy.9

commit v5 on v4

--- a/solution.py
+++ b/solution.py
@@ -459,12 +459,12 @@
         return carry
 
     lax.fori_loop(0, units, drain_right, 0)
+    lax.fori_loop(1, devices, drain_final, 0)
     lax.fori_loop(1, devices, wait_final, 0)
     smalls[3].wait()
     ladder = jnp.sum(parts[...], axis=0)
     for b in range(block_b):
         out[:, b, :] = res[:, b, :] + ladder[:, b * block_a : (b + 1) * block_a]
-    lax.fori_loop(1, devices, drain_final, 0)
 
 
 def local(sizes, amplitudes, pair_mask, left_factor, left_mask, right_factor, right_mask, residual_in):

time: 88.8 us -> 88.6 us (level)
  no operation moved by 1% of the time
where the time goes in v5:
time: 88.6 us; the launch traced here: 88.4 us
  Pallas kernels  87.8 us (99%)
    pallas_call x1, Pallas kernels, local(): pl.pallas_call(functools.partial(kernel, no, nv, na), out_shape=pltpu.VME...  87.8 us

profile of v5, /device:TPU:0, one launch (start us, length us, event | category | flops | bytes accessed | tf_op | source)
XLA Modules:
  0.0 88.4 jit_solution(18192457630542809940)
XLA Ops:
  0.0 87.8 %ladder.1 = f32[8,4,32]{2,1,0:T(4,128)S(1)} custom-call(s32[8,2,8]{2,1,0:T(2,128)} %pair_hbm.1, s32[2,8]{1,0:T(2,128)} %lmask_hbm.1, s32[8,8]{1,0:T(8,128)} %rmask_hbm.1, bf16[8,256,1024]{2,1,0:T(8,128)(2,1)} %amp_hbm.1, bf16[32,256,1024]{2,1,0:T(8,128)(2,1)} %left_hbm.1, bf16[128,4,1024]{2,1,0:T(4,128)(2,1)} %right_hbm.1, f32[8,4,32]{2,1,0:T(4,128)} %res_hbm.1), custom_call_target="tpu_custom_call" | custom-call | tf_op jit(solution)/shard_map/ladder/pallas_call | solution.py:486
  87.8 0.6 copy.9
